TPU v7x, 32 devices: a whole 2x2x4 slice. The times are simulated.
32 devices in a mesh: dp: 2 (over core), section: 4 (over z), mp: 4 (over y, x).
Axes of the slice: x: 2, y: 2, z: 4, core: 2. Of those that a mesh axis runs over, the one named last changes fastest.
Arguments:
- inputs: bfloat16 [48, 512], P(('dp', 'mp')), may hold values from -6 to 6
- tangents: bfloat16 [48, 32, 512], P(('dp', 'mp')), may hold values from -6 to 6
- targets: bfloat16 [48, 1024], P(('dp', 'mp')), may hold values from -24 to 24
- target_jac: bfloat16 [48, 32, 1024], P(('dp', 'mp')), may hold values from -24 to 24
- rank_mask: int32 [48, 32], P(('dp', 'mp')), may hold values from 0 to 1, as said below
- batch_order: int32 [8, 6], P(('dp', 'mp')), may hold values from 0 to 5, each once within a row
- encoder: bfloat16 [512, 2048], replicated, may hold values from -0.25 to 0.25
- layers: bfloat16 [4, 2048, 2048], P('section', 'mp'), may hold values from -0.125 to 0.125
- head_weight: bfloat16 [2048, 1024], replicated, may hold values from -0.125 to 0.125
Outputs:
- grad_layers: float32 [4, 2048, 2048], P('section', ('dp', 'mp'))
- grad_head: float32 [2048, 1024], P(('dp', 'mp'), 'section')
- loss_value: float32 [], replicated
Inputs may be any that keep to these rules, and one draw needn't show every extreme that they name: `rank_mask`: each sample's ones are its first 1 to 32 directions. `batch_order`: each row is an ordering of 0 .. 5.
All inputs are finite; a program needn't handle non-finite values.
Results may differ from a plain program's by a relative error of at most 0.035.
Values may be sent and summed in bfloat16 or wider, within the bound.
No kernel may reach another device: no remote copies, remote signals or barrier semaphores. Data moves between devices by JAX's collectives and lax.ppermute only.
A program may use at most 128 MiB of HBM per device.

v0:
```python
import jax
import jax.numpy as jnp
from jax import lax
from jax.sharding import PartitionSpec as P

MB = 6


def from_behind(value, axis, steps):
    count = lax.axis_size(axis)
    initial, last = (max(0, -steps), min(count, count - steps))
    return lax.ppermute(value, axis, [(source, source + steps) for source in range(initial, last)])


def forward_layer(row_block, weight):
    model_width = weight.shape[1]
    pre_act = jnp.dot(
        row_block.reshape(-1, model_width), weight, preferred_element_type=jnp.float32
    ).reshape(row_block.shape)
    tanh_p = jnp.tanh(pre_act[:, 0])
    slope_vals = 1.0 - tanh_p * tanh_p
    primal = row_block[:, 0].astype(jnp.float32) + tanh_p
    tangent = row_block[:, 1:].astype(jnp.float32) + slope_vals[:, None, :] * pre_act[:, 1:]
    return (jnp.concatenate([primal[:, None], tangent], axis=1).astype(jnp.bfloat16), pre_act)


def backward_layer(pre_act, grad_rows, weight):
    model_width = weight.shape[1]
    upstream = grad_rows.astype(jnp.float32)
    tanh_p = jnp.tanh(pre_act[:, 0])
    slope_vals = 1.0 - tanh_p * tanh_p
    tangent_part = upstream[:, 1:] * slope_vals[:, None, :]
    slope_grad = jnp.sum(upstream[:, 1:] * pre_act[:, 1:], axis=1)
    primal_part = upstream[:, 0] * slope_vals - 2.0 * slope_grad * tanh_p * slope_vals
    grad_mix = jnp.concatenate([primal_part[:, None], tangent_part], axis=1).astype(jnp.bfloat16)
    back_rows = jnp.dot(
        grad_mix.reshape(-1, model_width), weight.T, preferred_element_type=jnp.float32
    ).reshape(upstream.shape)
    return (grad_mix, (upstream + back_rows).astype(jnp.bfloat16))


def place_slot(store, value, batch_slot, is_valid):
    return lax.dynamic_update_index_in_dim(
        store, jnp.where(is_valid, value, store[batch_slot]), batch_slot, 0
    )


def local(
    inputs, tangents, targets, target_jac, rank_mask, batch_order, encoder, layers, head_weight
):
    samp_dev = inputs.shape[0]
    per_batch = samp_dev // MB
    row_depth = tangents.shape[1] + 1
    in_width = inputs.shape[1]
    model_width = layers.shape[2]
    out_width = head_weight.shape[1]
    sections = lax.axis_size("section")
    section_id = lax.axis_index("section")
    is_first = section_id == 0
    is_last = section_id == sections - 1
    layer_full = lax.all_gather(layers[0], "mp", axis=0, tiled=True)
    sample_order = batch_order[0]
    row_weight = jnp.concatenate(
        [jnp.ones((samp_dev, 1), jnp.float32), rank_mask.astype(jnp.float32)], axis=1
    )
    sample_total = jnp.sum(row_weight, axis=1)
    batch_counts = lax.psum(
        jnp.sum(sample_total[sample_order].reshape(MB, per_batch), axis=1), "mp"
    )

    def picked_of(batch_slot):
        return lax.dynamic_slice_in_dim(sample_order, batch_slot * per_batch, per_batch)

    def lift_batch(batch_slot):
        picked = picked_of(batch_slot)
        rows_in = jnp.concatenate([inputs[picked][:, None, :], tangents[picked]], axis=1)
        lifted = jnp.dot(rows_in.reshape(-1, in_width), encoder, preferred_element_type=jnp.float32)
        return lifted.reshape(per_batch, row_depth, model_width).astype(jnp.bfloat16)

    block_shape = (MB, per_batch, row_depth, model_width)
    pre_shape = (1, 1, 1, 1)

    def forward_tick(step_index, loop_state):
        incoming, store_in, store_pre, store_out = loop_state
        batch_index = step_index - section_id
        is_valid = (batch_index >= 0) & (batch_index < MB)
        batch_slot = jnp.clip(batch_index, 0, MB - 1)
        row_block = lax.cond(is_first, lambda: lift_batch(batch_slot), lambda: incoming)

        def forward_active():
            return forward_layer(row_block, layer_full)

        def forward_resting():
            return (row_block, jnp.zeros(row_block.shape, jnp.float32))

        layer_out, pre_act = lax.cond(is_valid, forward_active, forward_resting)
        store_in = place_slot(store_in, row_block, batch_slot, is_valid)
        store_out = place_slot(store_out, layer_out, batch_slot, is_valid)
        passed = from_behind(layer_out, "section", 1)
        return (passed, store_in, store_pre, store_out)

    start_state = (
        jnp.zeros(block_shape[1:], jnp.bfloat16),
        jnp.zeros(block_shape, jnp.bfloat16),
        jnp.zeros(pre_shape, jnp.float32),
        jnp.zeros(block_shape, jnp.bfloat16),
    )
    _, store_in, store_pre, store_out = lax.fori_loop(
        0, MB + sections - 1, forward_tick, start_state
    )

    def backward_tick(step_index, loop_state):
        incoming, store_mix, store_head, loss_acc = loop_state
        batch_index = step_index - (sections - 1 - section_id)
        is_valid = (batch_index >= 0) & (batch_index < MB)
        batch_slot = jnp.clip(batch_index, 0, MB - 1)
        batch_total = batch_counts[batch_slot]

        def head_part():
            final_rows = store_out[batch_slot]
            outputs = jnp.dot(
                final_rows.reshape(-1, model_width), head_weight, preferred_element_type=jnp.float32
            )
            outputs = outputs.reshape(per_batch, row_depth, out_width)
            picked = picked_of(batch_slot)
            wanted = jnp.concatenate(
                [targets[picked][:, None, :], target_jac[picked]], axis=1
            ).astype(jnp.float32)
            weights_here = row_weight[picked]
            mismatch = outputs - wanted
            misfit = jnp.sum(weights_here[:, :, None] * mismatch * mismatch) / batch_total
            cot_out = (2.0 * weights_here[:, :, None] * mismatch / batch_total).astype(jnp.bfloat16)
            grad_rows = jnp.dot(
                cot_out.reshape(-1, out_width), head_weight.T, preferred_element_type=jnp.float32
            )
            return (
                grad_rows.reshape(per_batch, row_depth, model_width).astype(jnp.bfloat16),
                cot_out,
                misfit,
            )

        def pass_on():
            return (
                incoming,
                jnp.zeros((per_batch, row_depth, out_width), jnp.bfloat16),
                jnp.zeros((), jnp.float32),
            )

        grad_rows, cot_out, misfit = lax.cond(is_last & is_valid, head_part, pass_on)

        def backward_active():
            row_block = store_in[batch_slot]
            pre_act = jnp.dot(
                row_block.reshape(-1, model_width), layer_full, preferred_element_type=jnp.float32
            ).reshape(row_block.shape)
            return backward_layer(pre_act, grad_rows, layer_full)

        def backward_resting():
            return (jnp.zeros(grad_rows.shape, jnp.bfloat16), grad_rows)

        grad_mix, grad_in = lax.cond(is_valid, backward_active, backward_resting)
        store_mix = place_slot(store_mix, grad_mix, batch_slot, is_valid)
        store_head = place_slot(store_head, cot_out, batch_slot, is_valid)
        loss_acc = loss_acc + jnp.where(is_valid, misfit, jnp.zeros((), jnp.float32))
        passed = from_behind(grad_in, "section", -1)
        return (passed, store_mix, store_head, loss_acc)

    back_state = (
        jnp.zeros(block_shape[1:], jnp.bfloat16),
        jnp.zeros(block_shape, jnp.bfloat16),
        jnp.zeros((MB, per_batch, row_depth, out_width), jnp.bfloat16),
        jnp.zeros((), jnp.float32),
    )
    _, store_mix, store_head, loss_acc = lax.fori_loop(
        0, MB + sections - 1, backward_tick, back_state
    )
    shard_rows = model_width // (lax.axis_size("dp") * lax.axis_size("mp"))
    in_flat = store_in.reshape(-1, model_width)
    mix_flat = store_mix.reshape(-1, model_width)
    grad_layers = lax.psum_scatter(
        jnp.dot(in_flat.T, mix_flat, preferred_element_type=jnp.float32).astype(jnp.bfloat16),
        ("dp", "mp"),
        scatter_dimension=0,
        tiled=True,
    ).astype(jnp.float32)[None]
    out_flat = store_out.reshape(-1, model_width)
    head_flat = store_head.reshape(-1, out_width)

    def compute():
        return jnp.dot(out_flat.T, head_flat, preferred_element_type=jnp.float32)

    def skipped():
        return jnp.zeros((lax.axis_size(("dp", "mp")) * shard_rows, out_width), jnp.float32)

    summed = lax.psum_scatter(
        lax.cond(is_last, compute, skipped).astype(jnp.bfloat16),
        ("dp", "mp"),
        scatter_dimension=0,
        tiled=True,
    )
    section_loss = lax.psum(loss_acc, ("dp", "mp"))
    loss_row = jnp.broadcast_to(section_loss, (1, sections))
    grad_head, loss_cols = (
        lax.psum_scatter(summed, "section", scatter_dimension=1, tiled=True).astype(jnp.float32),
        lax.psum_scatter(
            loss_row.astype(jnp.bfloat16), "section", scatter_dimension=1, tiled=True
        ).astype(jnp.float32),
    )
    loss_value = loss_cols[0, 0] / (lax.axis_size("dp") * MB * out_width)
    return (grad_layers, grad_head, loss_value)


def solution(mesh):
    in_specs = (
        P(("dp", "mp"), None),
        P(("dp", "mp"), None, None),
        P(("dp", "mp"), None),
        P(("dp", "mp"), None, None),
        P(("dp", "mp"), None),
        P(("dp", "mp"), None),
        P(),
        P("section", "mp", None),
        P(),
    )
    out_specs = (P("section", ("dp", "mp"), None), P(("dp", "mp"), "section"), P())
    return jax.shard_map(local, mesh=mesh, in_specs=in_specs, out_specs=out_specs, check_vma=False)
```

profile of v0, /device:TPU:0, one launch (start us, length us, event | category | flops | bytes accessed | tf_op | source)
XLA Modules:
  0.0 592.0 jit_solution(11319766208716329196)
XLA Ops:
  10.2 11.4 %psum.14 = f32[6]{0:T(128)S(1)} all-reduce(f32[6]{0:T(128)S(1)} %gather_fusion), channel_id=1, replica_groups=mesh['dp'=2,'section'=4,'mp'=4] {'mp'}, use_global_device_ids=true, to_apply=%region_7.0 | all-reduce | flops 6 | bytes 48 | tf_op jit(solution)/shard_map/psum | solution.py:67
  21.5 78.5 %all-gather.3.cloned.1.call-done = bf16[1,2048,2048]{2,1,0:T(8,128)(2,1)} async-done(((bf16[1,512,2048]{2,1,0:T(8,128)(2,1)}), bf16[1,2048,2048]{2,1,0:T(8,128)(2,1)}) %all-gather.3.cloned.1.call-update) | async-done | bytes 8388624 | tf_op jit(solution)/shard_map/all_gather | solution.py:61
  101.9 119.8 %while.49 = (s32[]{:T(128)}, bf16[1,33,2048]{2,1,0:T(8,128)(2,1)}, bf16[6,1,33,2048]{3,2,1,0:T(8,128)(2,1)S(1)}, bf16[6,1,33,2048]{3,2,1,0:T(8,128)(2,1)}, s32[]...) while((s32[]{:T(128)}, bf16[1,33,2048]{2,1,0:T(8,128)(2,1)}, ...), condition=%wide.region_5.0_spmd, body=%wide.region_0.5_spmd.sunk | while | flops 346843136 | bytes 14290849 | solution.py:108
  194.4 6.0 %collective-permute-start = (bf16[1,33,2048]{2,1,0:T(8,128)(2,1)S(1)}, bf16[1,33,2048]{2,1,0:T(8,128)(2,1)}, u32[]{:S(2)}, u32[]{:S(2)}) collective-permute-start(bf16[1,33,2048]{2,1,0:T(8,128)(2,1)S(1)} %get-tuple-element.1090), channel_id=1, source_target_pairs={{0,4},{4,8},{8,12},{1,5},{5,9},{9,13},{2,6},{6,10},{10,14},{3,7},{... | collective-permute-start | bytes 405512 | tf_op jit(solution)/shard_map/while/body/eval_jaxpr/ppermute | solution.py:12
  221.9 212.5 %while.50 = (s32[]{:T(128)}, bf16[1,33,2048]{2,1,0:T(8,128)(2,1)S(1)}, bf16[6,1,33,2048]{3,2,1,0:T(8,128)(2,1)S(1)}, bf16[6,1,33,1024]{3,2,1,0:T(8,128)(2,1)S(1)...) while((s32[]{:T(128)}, ...), condition=%wide.region_15.16_spmd, body=%wide.region_8.15_spmd.sunk | while | flops 832231424 | bytes 80709456 | solution.py:174
  224.1 6.3 %collective-permute-done.1 = bf16[1,33,2048]{2,1,0:T(8,128)(2,1)S(1)} collective-permute-done((bf16[1,33,2048]{2,1,0:T(8,128)(2,1)S(1)}, bf16[1,33,2048]{2,1,0:T(8,128)(2,1)S(1)}, u32[]{:S(2)}, u32[]{:S(2)}) %collective-permute-start.1) | collective-permute-done | bytes 135200 | tf_op jit(solution)/shard_map/while/body/eval_jaxpr/ppermute | solution.py:12
  232.6 8.7 %collective-permute-done.1 = bf16[1,33,2048]{2,1,0:T(8,128)(2,1)S(1)} collective-permute-done((bf16[1,33,2048]{2,1,0:T(8,128)(2,1)S(1)}, bf16[1,33,2048]{2,1,0:T(8,128)(2,1)S(1)}, u32[]{:S(2)}, u32[]{:S(2)}) %collective-permute-start.1) | collective-permute-done | bytes 135200 | tf_op jit(solution)/shard_map/while/body/eval_jaxpr/ppermute | solution.py:12
  243.4 43.9 %collective-permute-done.1 = bf16[1,33,2048]{2,1,0:T(8,128)(2,1)S(1)} collective-permute-done((bf16[1,33,2048]{2,1,0:T(8,128)(2,1)S(1)}, bf16[1,33,2048]{2,1,0:T(8,128)(2,1)S(1)}, u32[]{:S(2)}, u32[]{:S(2)}) %collective-permute-start.1) | collective-permute-done | bytes 135200 | tf_op jit(solution)/shard_map/while/body/eval_jaxpr/ppermute | solution.py:12
  288.0 8.5 %conditional.13 = (bf16[1,33,2048]{2,1,0:T(8,128)(2,1)S(1)}, bf16[1,33,2048]{2,1,0:T(8,128)(2,1)S(1)}) conditional(s32[]{:T(128)} %convert_element_type.140, bf16[1,33,2048]{2,1,0:T(8,128)(2,1)S(1)} %get-tuple-element.965, (bf16[1,33,2048]{2,1,0:T(8,128)(2,1)S(1)}, s32[]{:T(128)}, bf16[6,1,33,2048]{3,2,1,0:T(8,128)(2,1)S(1)}, ...), branch_computations={%region_12.12_spmd, %region_13.14_spmd} | conditional | flops 554866688 | bytes 53235792 | solution.py:161
  298.8 14.7 %collective-permute-done.1 = bf16[1,33,2048]{2,1,0:T(8,128)(2,1)S(1)} collective-permute-done((bf16[1,33,2048]{2,1,0:T(8,128)(2,1)S(1)}, bf16[1,33,2048]{2,1,0:T(8,128)(2,1)S(1)}, u32[]{:S(2)}, u32[]{:S(2)}) %collective-permute-start.1) | collective-permute-done | bytes 135200 | tf_op jit(solution)/shard_map/while/body/eval_jaxpr/ppermute | solution.py:12
  314.1 8.5 %conditional.13 = (bf16[1,33,2048]{2,1,0:T(8,128)(2,1)S(1)}, bf16[1,33,2048]{2,1,0:T(8,128)(2,1)S(1)}) conditional(s32[]{:T(128)} %convert_element_type.140, bf16[1,33,2048]{2,1,0:T(8,128)(2,1)S(1)} %get-tuple-element.965, (bf16[1,33,2048]{2,1,0:T(8,128)(2,1)S(1)}, s32[]{:T(128)}, bf16[6,1,33,2048]{3,2,1,0:T(8,128)(2,1)S(1)}, ...), branch_computations={%region_12.12_spmd, %region_13.14_spmd} | conditional | flops 554866688 | bytes 53235792 | solution.py:161
  325.0 14.7 %collective-permute-done.1 = bf16[1,33,2048]{2,1,0:T(8,128)(2,1)S(1)} collective-permute-done((bf16[1,33,2048]{2,1,0:T(8,128)(2,1)S(1)}, bf16[1,33,2048]{2,1,0:T(8,128)(2,1)S(1)}, u32[]{:S(2)}, u32[]{:S(2)}) %collective-permute-start.1) | collective-permute-done | bytes 135200 | tf_op jit(solution)/shard_map/while/body/eval_jaxpr/ppermute | solution.py:12
  340.3 8.5 %conditional.13 = (bf16[1,33,2048]{2,1,0:T(8,128)(2,1)S(1)}, bf16[1,33,2048]{2,1,0:T(8,128)(2,1)S(1)}) conditional(s32[]{:T(128)} %convert_element_type.140, bf16[1,33,2048]{2,1,0:T(8,128)(2,1)S(1)} %get-tuple-element.965, (bf16[1,33,2048]{2,1,0:T(8,128)(2,1)S(1)}, s32[]{:T(128)}, bf16[6,1,33,2048]{3,2,1,0:T(8,128)(2,1)S(1)}, ...), branch_computations={%region_12.12_spmd, %region_13.14_spmd} | conditional | flops 554866688 | bytes 53235792 | solution.py:161
  351.1 14.7 %collective-permute-done.1 = bf16[1,33,2048]{2,1,0:T(8,128)(2,1)S(1)} collective-permute-done((bf16[1,33,2048]{2,1,0:T(8,128)(2,1)S(1)}, bf16[1,33,2048]{2,1,0:T(8,128)(2,1)S(1)}, u32[]{:S(2)}, u32[]{:S(2)}) %collective-permute-start.1) | collective-permute-done | bytes 135200 | tf_op jit(solution)/shard_map/while/body/eval_jaxpr/ppermute | solution.py:12
  366.4 8.5 %conditional.13 = (bf16[1,33,2048]{2,1,0:T(8,128)(2,1)S(1)}, bf16[1,33,2048]{2,1,0:T(8,128)(2,1)S(1)}) conditional(s32[]{:T(128)} %convert_element_type.140, bf16[1,33,2048]{2,1,0:T(8,128)(2,1)S(1)} %get-tuple-element.965, (bf16[1,33,2048]{2,1,0:T(8,128)(2,1)S(1)}, s32[]{:T(128)}, bf16[6,1,33,2048]{3,2,1,0:T(8,128)(2,1)S(1)}, ...), branch_computations={%region_12.12_spmd, %region_13.14_spmd} | conditional | flops 554866688 | bytes 53235792 | solution.py:161
  377.2 14.7 %collective-permute-done.1 = bf16[1,33,2048]{2,1,0:T(8,128)(2,1)S(1)} collective-permute-done((bf16[1,33,2048]{2,1,0:T(8,128)(2,1)S(1)}, bf16[1,33,2048]{2,1,0:T(8,128)(2,1)S(1)}, u32[]{:S(2)}, u32[]{:S(2)}) %collective-permute-start.1) | collective-permute-done | bytes 135200 | tf_op jit(solution)/shard_map/while/body/eval_jaxpr/ppermute | solution.py:12
  392.6 8.5 %conditional.13 = (bf16[1,33,2048]{2,1,0:T(8,128)(2,1)S(1)}, bf16[1,33,2048]{2,1,0:T(8,128)(2,1)S(1)}) conditional(s32[]{:T(128)} %convert_element_type.140, bf16[1,33,2048]{2,1,0:T(8,128)(2,1)S(1)} %get-tuple-element.965, (bf16[1,33,2048]{2,1,0:T(8,128)(2,1)S(1)}, s32[]{:T(128)}, bf16[6,1,33,2048]{3,2,1,0:T(8,128)(2,1)S(1)}, ...), branch_computations={%region_12.12_spmd, %region_13.14_spmd} | conditional | flops 554866688 | bytes 53235792 | solution.py:161
  403.4 14.7 %collective-permute-done.1 = bf16[1,33,2048]{2,1,0:T(8,128)(2,1)S(1)} collective-permute-done((bf16[1,33,2048]{2,1,0:T(8,128)(2,1)S(1)}, bf16[1,33,2048]{2,1,0:T(8,128)(2,1)S(1)}, u32[]{:S(2)}, u32[]{:S(2)}) %collective-permute-start.1) | collective-permute-done | bytes 135200 | tf_op jit(solution)/shard_map/while/body/eval_jaxpr/ppermute | solution.py:12
  418.7 8.5 %conditional.13 = (bf16[1,33,2048]{2,1,0:T(8,128)(2,1)S(1)}, bf16[1,33,2048]{2,1,0:T(8,128)(2,1)S(1)}) conditional(s32[]{:T(128)} %convert_element_type.140, bf16[1,33,2048]{2,1,0:T(8,128)(2,1)S(1)} %get-tuple-element.965, (bf16[1,33,2048]{2,1,0:T(8,128)(2,1)S(1)}, s32[]{:T(128)}, bf16[6,1,33,2048]{3,2,1,0:T(8,128)(2,1)S(1)}, ...), branch_computations={%region_12.12_spmd, %region_13.14_spmd} | conditional | flops 554866688 | bytes 53235792 | solution.py:161
  437.0 48.5 %reduce-scatter.7.cloned.1.call-done = bf16[256,1024]{1,0:T(8,128)(2,1)} async-done(((bf16[2048,1024]{1,0:T(8,128)(2,1)}), bf16[256,1024]{1,0:T(8,128)(2,1)}) %reduce-scatter.7.cloned.1.call-update) | async-done | bytes 524304 | tf_op jit(solution)/shard_map/reduce_scatter | solution.py:195
  485.7 5.6 bitcast_convert_fusion
  492.5 15.4 %psum.15 = bf16[]{:T(256)} all-reduce(f32[]{:T(128)} %get-tuple-element.664), channel_id=1, replica_groups=mesh['dp'=2,'section'=4,'mp'=4] {'dp','mp'}, use_global_device_ids=true, to_apply=%region_21.22 | all-reduce | flops 1 | bytes 6 | tf_op jit(solution)/shard_map/psum | solution.py:201
  508.6 12.1 %all-reduce.1 = bf16[1,4]{1,0:T(2,128)(2,1)S(1)} all-reduce(bf16[1,4]{1,0:T(2,128)(2,1)S(1)} %broadcast_in_dim.72), channel_id=6, replica_groups=mesh['dp'=2,'section'=4,'mp'=4] {'section'}, use_global_device_ids=true, to_apply=%region_22.23.clone | all-reduce | flops 4 | bytes 16
  523.6 59.1 %reduce-scatter.5.cloned.1.call-done = bf16[256,2048]{1,0:T(8,128)(2,1)} async-done(((bf16[2048,2048]{1,0:T(8,128)(2,1)}), bf16[256,2048]{1,0:T(8,128)(2,1)}) %reduce-scatter.5.cloned.1.call-update) | async-done | bytes 1048592 | tf_op jit(solution)/shard_map/reduce_scatter | solution.py:180
  (306 shorter events, 269.7 us)
Async XLA Ops:
  7.2 94.8 %copy-start.3 = (s32[1,6]{1,0:T(1,128)S(1)}, s32[1,6]{1,0:T(1,128)}, u32[]{:S(2)}) copy-start(s32[1,6]{1,0:T(1,128)} %param.28) | copy-start | bytes 76
  7.2 94.8 %copy-start.2 = (bf16[512,2048]{1,0:T(8,128)(2,1)S(1)}, bf16[512,2048]{1,0:T(8,128)(2,1)}, u32[]{:S(2)}) copy-start(bf16[512,2048]{1,0:T(8,128)(2,1)} %param.29) | copy-start | bytes 6291460
  7.2 92.9 %all-gather.3.cloned.1.call-start = ((), (), s32[]{:S(2)}) async-start(), calls=%async_computation.6 | async-start | bytes 10485760 | tf_op jit(solution)/shard_map/all_gather | solution.py:61
  7.9 477.5 %reduce-scatter.7.cloned.1.call-start = ((), (), s32[]{:S(2)}) async-start(), calls=%async_computation.4 | async-start | bytes 4718592 | tf_op jit(solution)/shard_map/reduce_scatter | solution.py:195
  112.2 4.9 collective-permute-start
  127.4 4.3 collective-permute-start
  141.9 4.1 collective-permute-start
  156.3 4.1 collective-permute-start
  170.7 4.1 collective-permute-start
  185.1 4.1 collective-permute-start
  194.4 8.1 %collective-permute-start = (bf16[1,33,2048]{2,1,0:T(8,128)(2,1)S(1)}, bf16[1,33,2048]{2,1,0:T(8,128)(2,1)}, u32[]{:S(2)}, u32[]{:S(2)}) collective-permute-start(bf16[1,33,2048]{2,1,0:T(8,128)(2,1)S(1)} %get-tuple-element.1090), channel_id=1, source_target_pairs={{0,4},{4,8},{8,12},{1,5},{5,9},{9,13},{2,6},{6,10},{10,14},{3,7},{... | collective-permute-start | bytes 405512 | tf_op jit(solution)/shard_map/while/body/eval_jaxpr/ppermute | solution.py:12
  207.8 4.1 collective-permute-start
  217.1 4.6 collective-permute-start
  222.6 7.8 %collective-permute-start.1 = (bf16[1,33,2048]{2,1,0:T(8,128)(2,1)S(1)}, bf16[1,33,2048]{2,1,0:T(8,128)(2,1)S(1)}, u32[]{:S(2)}, u32[]{:S(2)}) collective-permute-start(bf16[1,33,2048]{2,1,0:T(8,128)(2,1)S(1)} %get-tuple-element.966), channel_id=1, source_target_pairs={{4,0},{8,4},{12,8},{5,1},{9,5},{13,9},{6,2},{10,6},{14,10},{7,3},{... | collective-permute-start | bytes 405512 | tf_op jit(solution)/shard_map/while/body/eval_jaxpr/ppermute | solution.py:12
  231.1 10.2 %collective-permute-start.1 = (bf16[1,33,2048]{2,1,0:T(8,128)(2,1)S(1)}, bf16[1,33,2048]{2,1,0:T(8,128)(2,1)S(1)}, u32[]{:S(2)}, u32[]{:S(2)}) collective-permute-start(bf16[1,33,2048]{2,1,0:T(8,128)(2,1)S(1)} %get-tuple-element.966), channel_id=1, source_target_pairs={{4,0},{8,4},{12,8},{5,1},{9,5},{13,9},{6,2},{10,6},{14,10},{7,3},{... | collective-permute-start | bytes 405512 | tf_op jit(solution)/shard_map/while/body/eval_jaxpr/ppermute | solution.py:12
  242.0 45.4 %collective-permute-start.1 = (bf16[1,33,2048]{2,1,0:T(8,128)(2,1)S(1)}, bf16[1,33,2048]{2,1,0:T(8,128)(2,1)S(1)}, u32[]{:S(2)}, u32[]{:S(2)}) collective-permute-start(bf16[1,33,2048]{2,1,0:T(8,128)(2,1)S(1)} %get-tuple-element.966), channel_id=1, source_target_pairs={{4,0},{8,4},{12,8},{5,1},{9,5},{13,9},{6,2},{10,6},{14,10},{7,3},{... | collective-permute-start | bytes 405512 | tf_op jit(solution)/shard_map/while/body/eval_jaxpr/ppermute | solution.py:12
  296.5 17.0 %collective-permute-start.1 = (bf16[1,33,2048]{2,1,0:T(8,128)(2,1)S(1)}, bf16[1,33,2048]{2,1,0:T(8,128)(2,1)S(1)}, u32[]{:S(2)}, u32[]{:S(2)}) collective-permute-start(bf16[1,33,2048]{2,1,0:T(8,128)(2,1)S(1)} %get-tuple-element.966), channel_id=1, source_target_pairs={{4,0},{8,4},{12,8},{5,1},{9,5},{13,9},{6,2},{10,6},{14,10},{7,3},{... | collective-permute-start | bytes 405512 | tf_op jit(solution)/shard_map/while/body/eval_jaxpr/ppermute | solution.py:12
  322.6 17.0 %collective-permute-start.1 = (bf16[1,33,2048]{2,1,0:T(8,128)(2,1)S(1)}, bf16[1,33,2048]{2,1,0:T(8,128)(2,1)S(1)}, u32[]{:S(2)}, u32[]{:S(2)}) collective-permute-start(bf16[1,33,2048]{2,1,0:T(8,128)(2,1)S(1)} %get-tuple-element.966), channel_id=1, source_target_pairs={{4,0},{8,4},{12,8},{5,1},{9,5},{13,9},{6,2},{10,6},{14,10},{7,3},{... | collective-permute-start | bytes 405512 | tf_op jit(solution)/shard_map/while/body/eval_jaxpr/ppermute | solution.py:12
  348.8 17.0 %collective-permute-start.1 = (bf16[1,33,2048]{2,1,0:T(8,128)(2,1)S(1)}, bf16[1,33,2048]{2,1,0:T(8,128)(2,1)S(1)}, u32[]{:S(2)}, u32[]{:S(2)}) collective-permute-start(bf16[1,33,2048]{2,1,0:T(8,128)(2,1)S(1)} %get-tuple-element.966), channel_id=1, source_target_pairs={{4,0},{8,4},{12,8},{5,1},{9,5},{13,9},{6,2},{10,6},{14,10},{7,3},{... | collective-permute-start | bytes 405512 | tf_op jit(solution)/shard_map/while/body/eval_jaxpr/ppermute | solution.py:12
  374.9 17.0 %collective-permute-start.1 = (bf16[1,33,2048]{2,1,0:T(8,128)(2,1)S(1)}, bf16[1,33,2048]{2,1,0:T(8,128)(2,1)S(1)}, u32[]{:S(2)}, u32[]{:S(2)}) collective-permute-start(bf16[1,33,2048]{2,1,0:T(8,128)(2,1)S(1)} %get-tuple-element.966), channel_id=1, source_target_pairs={{4,0},{8,4},{12,8},{5,1},{9,5},{13,9},{6,2},{10,6},{14,10},{7,3},{... | collective-permute-start | bytes 405512 | tf_op jit(solution)/shard_map/while/body/eval_jaxpr/ppermute | solution.py:12
  401.1 17.0 %collective-permute-start.1 = (bf16[1,33,2048]{2,1,0:T(8,128)(2,1)S(1)}, bf16[1,33,2048]{2,1,0:T(8,128)(2,1)S(1)}, u32[]{:S(2)}, u32[]{:S(2)}) collective-permute-start(bf16[1,33,2048]{2,1,0:T(8,128)(2,1)S(1)} %get-tuple-element.966), channel_id=1, source_target_pairs={{4,0},{8,4},{12,8},{5,1},{9,5},{13,9},{6,2},{10,6},{14,10},{7,3},{... | collective-permute-start | bytes 405512 | tf_op jit(solution)/shard_map/while/body/eval_jaxpr/ppermute | solution.py:12
  427.2 7.2 %collective-permute-start.1 = (bf16[1,33,2048]{2,1,0:T(8,128)(2,1)S(1)}, bf16[1,33,2048]{2,1,0:T(8,128)(2,1)S(1)}, u32[]{:S(2)}, u32[]{:S(2)}) collective-permute-start(bf16[1,33,2048]{2,1,0:T(8,128)(2,1)S(1)} %get-tuple-element.966), channel_id=1, source_target_pairs={{4,0},{8,4},{12,8},{5,1},{9,5},{13,9},{6,2},{10,6},{14,10},{7,3},{... | collective-permute-start | bytes 405512 | tf_op jit(solution)/shard_map/while/body/eval_jaxpr/ppermute | solution.py:12
  436.9 85.0 %reduce-scatter.9.cloned.1.call-start = ((), (), s32[]{:S(2)}) async-start(), calls=%async_computation.5 | async-start | bytes 655360 | tf_op jit(solution)/shard_map/reduce_scatter | solution.py:204
  485.5 97.2 %reduce-scatter.5.cloned.1.call-start = ((), (), s32[]{:S(2)}) async-start(), calls=%async_computation.3 | async-start | bytes 9437184 | tf_op jit(solution)/shard_map/reduce_scatter | solution.py:180
  (7 other events, 35.3 us)
Sparse Core Ops, SparseCore 0:
  9.8 90.1 all-gather.2
  437.0 48.3 reduce-scatter.6
  487.7 21.8 reduce-scatter.8
  512.9 69.6 reduce-scatter.4
where the time goes:
time: 595 us; the launch traced here: 592 us
  waiting for transfers between devices  329 us (55%)
  matrix products  85.4 us (14%)
  local copies, waits for them, and re-layouts  51.3 us (9%)
  blocking collectives  38.9 us (7%)
  starting transfers between devices  34.3 us (6%)
  other arithmetic  22.6 us (4%)
  loops' own time  16.8 us (3%)
  between operations  13.8 us (2%)
    ppermute x18, waiting for transfers between devices, from_behind(): lax.ppermute(value, axis, [(source, source + steps) for source in range(i...  142 us
    all_gather x1, waiting for transfers between devices, local(): layer_full = lax.all_gather(layers[0], 'mp', axis=0, tiled=True)  78.5 us
    reduce_scatter x1, waiting for transfers between devices, local(): lax.psum_scatter(jnp.dot(in_flat.T, mix_flat, preferred_element_type=jnp....  59.1 us
    reduce_scatter x1, waiting for transfers between devices, local(): lax.psum_scatter(lax.cond(is_last, compute, skipped).astype(jnp.bfloat16)...  48.5 us
    ppermute x18, starting transfers between devices, from_behind(): lax.ppermute(value, axis, [(source, source + steps) for source in range(i...  33.9 us
    dot_general x6, matrix products, backward_active(): jnp.dot(row_block.reshape(-1, model_width), layer_full, preferred_element...  30.4 us
    dot_general x6, matrix products, forward_layer(): jnp.dot(row_block.reshape(-1, model_width), weight, preferred_element_typ...  29.5 us
    another operation x27, local copies, waits for them, and re-layouts  18.5 us
  transfers between devices with their start and end apart: 22, of which 21 were waited for; matrix products, arithmetic and copies ran while one was open for 6% of the time, Pallas kernels for 0%

commit v1 on v0

--- a/solution.py
+++ b/solution.py
@@ -58,7 +58,9 @@
     section_id = lax.axis_index("section")
     is_first = section_id == 0
     is_last = section_id == sections - 1
-    layer_full = lax.all_gather(layers[0], "mp", axis=0, tiled=True)
+    block = layers[0]
+    stack = jnp.stack([block] * lax.axis_size("mp"))
+    layer_full = jnp.concatenate(lax.all_to_all(stack, "mp", 0, 0), axis=0)
     sample_order = batch_order[0]
     row_weight = jnp.concatenate(
         [jnp.ones((samp_dev, 1), jnp.float32), rank_mask.astype(jnp.float32)], axis=1

time: 595 us -> 638 us (1.072)
  blocking collectives: 38.9 us -> 124 us
  waiting for transfers between devices: 329 us -> 258 us
  matrix products: 85.4 us -> 105 us
    psum x1, blocking collectives: 11.4 us -> 96 us  [local(): lax.psum(jnp.sum(sample_total[sample_order].reshape(MB, per_batch), axis=...]
    all_gather x1 -> x0, waiting for transfers between devices: 78.5 us -> none  [local(): layer_full = lax.all_gather(layers[0], 'mp', axis=0, tiled=True)]
    dot_general x6, matrix products: 15.6 us -> 35.8 us  [backward_layer(): jnp.dot(grad_mix.reshape(-1, model_width), weight.T, preferred_element_ty...]
    ppermute x18, waiting for transfers between devices: 142 us -> 150 us  [from_behind(): lax.ppermute(value, axis, [(source, source + steps) for source in range(i...]
    another operation x27 -> x28, local copies, waits for them, and re-layouts: 18.5 us -> 24.4 us
  transfers between devices with their start and end apart: 22 -> 22, of which waited for: 21 -> 20; matrix products, arithmetic and copies ran while one was open for 6% -> 5% of each run, Pallas kernels for 0% -> 0%
where the time goes in v1:
time: 638 us; the launch traced here: 635 us
  waiting for transfers between devices  258 us (40%)
  blocking collectives  124 us (19%)
  matrix products  105 us (16%)
  local copies, waits for them, and re-layouts  54.9 us (9%)
  starting transfers between devices  40.3 us (6%)
  other arithmetic  21.3 us (3%)
  loops' own time  18.2 us (3%)
  between operations  13.8 us (2%)
    ppermute x18, waiting for transfers between devices, from_behind(): lax.ppermute(value, axis, [(source, source + steps) for source in range(i...  150 us
    psum x1, blocking collectives, local(): lax.psum(jnp.sum(sample_total[sample_order].reshape(MB, per_batch), axis=...  96 us
    reduce_scatter x1, waiting for transfers between devices, local(): lax.psum_scatter(jnp.dot(in_flat.T, mix_flat, preferred_element_type=jnp....  59.3 us
    reduce_scatter x1, waiting for transfers between devices, local(): lax.psum_scatter(lax.cond(is_last, compute, skipped).astype(jnp.bfloat16)...  48.6 us
    dot_general x6, matrix products, backward_layer(): jnp.dot(grad_mix.reshape(-1, model_width), weight.T, preferred_element_ty...  35.8 us
    ppermute x18, starting transfers between devices, from_behind(): lax.ppermute(value, axis, [(source, source + steps) for source in range(i...  34.2 us
    dot_general x6, matrix products, forward_layer(): jnp.dot(row_block.reshape(-1, model_width), weight, preferred_element_typ...  29.5 us
    dot_general x6, matrix products, backward_active(): jnp.dot(row_block.reshape(-1, model_width), layer_full, preferred_element...  29.5 us
  transfers between devices with their start and end apart: 22, of which 20 were waited for; matrix products, arithmetic and copies ran while one was open for 5% of the time, Pallas kernels for 0%

profile of v1, /device:TPU:0, one launch (start us, length us, event | category | flops | bytes accessed | tf_op | source)
XLA Modules:
  0.0 634.8 jit_solution(2145048887419913694)
XLA Ops:
  19.8 96.0 %psum.14 = f32[6]{0:T(128)S(1)} all-reduce(f32[6]{0:T(128)S(1)} %gather_fusion), channel_id=1, replica_groups=mesh['dp'=2,'section'=4,'mp'=4] {'mp'}, use_global_device_ids=true, to_apply=%region_7.0 | all-reduce | flops 6 | bytes 48 | tf_op jit(solution)/shard_map/psum | solution.py:69
  117.7 121.0 %while.49 = (s32[]{:T(128)}, bf16[1,33,2048]{2,1,0:T(8,128)(2,1)}, bf16[6,1,33,2048]{3,2,1,0:T(8,128)(2,1)S(1)}, bf16[6,1,33,2048]{3,2,1,0:T(8,128)(2,1)}, s32[]...) while((s32[]{:T(128)}, bf16[1,33,2048]{2,1,0:T(8,128)(2,1)}, ...), condition=%wide.region_5.0_spmd, body=%wide.region_0.5_spmd.sunk | while | flops 346843136 | bytes 14290849 | solution.py:110
  238.8 238.0 %while.50 = (s32[]{:T(128)}, bf16[1,33,2048]{2,1,0:T(8,128)(2,1)S(1)}, bf16[6,1,33,2048]{3,2,1,0:T(8,128)(2,1)S(1)}, bf16[6,1,33,1024]{3,2,1,0:T(8,128)(2,1)S(1)...) while((s32[]{:T(128)}, ...), condition=%wide.region_15.16_spmd, body=%wide.region_8.15_spmd.sunk | while | flops 832231424 | bytes 47154988 | solution.py:176
  241.0 6.8 %collective-permute-done.1 = bf16[1,33,2048]{2,1,0:T(8,128)(2,1)S(1)} collective-permute-done((bf16[1,33,2048]{2,1,0:T(8,128)(2,1)S(1)}, bf16[1,33,2048]{2,1,0:T(8,128)(2,1)S(1)}, u32[]{:S(2)}, u32[]{:S(2)}) %collective-permute-start.1) | collective-permute-done | bytes 135200 | tf_op jit(solution)/shard_map/while/body/eval_jaxpr/ppermute | solution.py:12
  250.0 7.4 %collective-permute-done.1 = bf16[1,33,2048]{2,1,0:T(8,128)(2,1)S(1)} collective-permute-done((bf16[1,33,2048]{2,1,0:T(8,128)(2,1)S(1)}, bf16[1,33,2048]{2,1,0:T(8,128)(2,1)S(1)}, u32[]{:S(2)}, u32[]{:S(2)}) %collective-permute-start.1) | collective-permute-done | bytes 135200 | tf_op jit(solution)/shard_map/while/body/eval_jaxpr/ppermute | solution.py:12
  259.5 52.5 %collective-permute-done.1 = bf16[1,33,2048]{2,1,0:T(8,128)(2,1)S(1)} collective-permute-done((bf16[1,33,2048]{2,1,0:T(8,128)(2,1)S(1)}, bf16[1,33,2048]{2,1,0:T(8,128)(2,1)S(1)}, u32[]{:S(2)}, u32[]{:S(2)}) %collective-permute-start.1) | collective-permute-done | bytes 135200 | tf_op jit(solution)/shard_map/while/body/eval_jaxpr/ppermute | solution.py:12
  312.6 11.2 %conditional.13 = (bf16[1,33,2048]{2,1,0:T(8,128)(2,1)S(1)}, bf16[1,33,2048]{2,1,0:T(8,128)(2,1)S(1)}) conditional(s32[]{:T(128)} %convert_element_type.140, bf16[1,33,2048]{2,1,0:T(8,128)(2,1)S(1)} %get-tuple-element.965, (bf16[1,33,2048]{2,1,0:T(8,128)(2,1)S(1)}, s32[]{:T(128)}, bf16[6,1,33,2048]{3,2,1,0:T(8,128)(2,1)S(1)}, ...), branch_computations={%region_12.12_spmd, %region_13.14_spmd} | conditional | flops 554866688 | bytes 19681334 | solution.py:163
  317.7 6.0 fusion.4
  326.1 15.0 %collective-permute-done.1 = bf16[1,33,2048]{2,1,0:T(8,128)(2,1)S(1)} collective-permute-done((bf16[1,33,2048]{2,1,0:T(8,128)(2,1)S(1)}, bf16[1,33,2048]{2,1,0:T(8,128)(2,1)S(1)}, u32[]{:S(2)}, u32[]{:S(2)}) %collective-permute-start.1) | collective-permute-done | bytes 135200 | tf_op jit(solution)/shard_map/while/body/eval_jaxpr/ppermute | solution.py:12
  341.7 11.2 %conditional.13 = (bf16[1,33,2048]{2,1,0:T(8,128)(2,1)S(1)}, bf16[1,33,2048]{2,1,0:T(8,128)(2,1)S(1)}) conditional(s32[]{:T(128)} %convert_element_type.140, bf16[1,33,2048]{2,1,0:T(8,128)(2,1)S(1)} %get-tuple-element.965, (bf16[1,33,2048]{2,1,0:T(8,128)(2,1)S(1)}, s32[]{:T(128)}, bf16[6,1,33,2048]{3,2,1,0:T(8,128)(2,1)S(1)}, ...), branch_computations={%region_12.12_spmd, %region_13.14_spmd} | conditional | flops 554866688 | bytes 19681334 | solution.py:163
  346.9 6.0 fusion.4
  355.3 15.0 %collective-permute-done.1 = bf16[1,33,2048]{2,1,0:T(8,128)(2,1)S(1)} collective-permute-done((bf16[1,33,2048]{2,1,0:T(8,128)(2,1)S(1)}, bf16[1,33,2048]{2,1,0:T(8,128)(2,1)S(1)}, u32[]{:S(2)}, u32[]{:S(2)}) %collective-permute-start.1) | collective-permute-done | bytes 135200 | tf_op jit(solution)/shard_map/while/body/eval_jaxpr/ppermute | solution.py:12
  370.9 11.2 %conditional.13 = (bf16[1,33,2048]{2,1,0:T(8,128)(2,1)S(1)}, bf16[1,33,2048]{2,1,0:T(8,128)(2,1)S(1)}) conditional(s32[]{:T(128)} %convert_element_type.140, bf16[1,33,2048]{2,1,0:T(8,128)(2,1)S(1)} %get-tuple-element.965, (bf16[1,33,2048]{2,1,0:T(8,128)(2,1)S(1)}, s32[]{:T(128)}, bf16[6,1,33,2048]{3,2,1,0:T(8,128)(2,1)S(1)}, ...), branch_computations={%region_12.12_spmd, %region_13.14_spmd} | conditional | flops 554866688 | bytes 19681334 | solution.py:163
  384.5 15.0 %collective-permute-done.1 = bf16[1,33,2048]{2,1,0:T(8,128)(2,1)S(1)} collective-permute-done((bf16[1,33,2048]{2,1,0:T(8,128)(2,1)S(1)}, bf16[1,33,2048]{2,1,0:T(8,128)(2,1)S(1)}, u32[]{:S(2)}, u32[]{:S(2)}) %collective-permute-start.1) | collective-permute-done | bytes 135200 | tf_op jit(solution)/shard_map/while/body/eval_jaxpr/ppermute | solution.py:12
  400.1 11.2 %conditional.13 = (bf16[1,33,2048]{2,1,0:T(8,128)(2,1)S(1)}, bf16[1,33,2048]{2,1,0:T(8,128)(2,1)S(1)}) conditional(s32[]{:T(128)} %convert_element_type.140, bf16[1,33,2048]{2,1,0:T(8,128)(2,1)S(1)} %get-tuple-element.965, (bf16[1,33,2048]{2,1,0:T(8,128)(2,1)S(1)}, s32[]{:T(128)}, bf16[6,1,33,2048]{3,2,1,0:T(8,128)(2,1)S(1)}, ...), branch_computations={%region_12.12_spmd, %region_13.14_spmd} | conditional | flops 554866688 | bytes 19681334 | solution.py:163
  405.2 6.0 fusion.4
  413.6 15.0 %collective-permute-done.1 = bf16[1,33,2048]{2,1,0:T(8,128)(2,1)S(1)} collective-permute-done((bf16[1,33,2048]{2,1,0:T(8,128)(2,1)S(1)}, bf16[1,33,2048]{2,1,0:T(8,128)(2,1)S(1)}, u32[]{:S(2)}, u32[]{:S(2)}) %collective-permute-start.1) | collective-permute-done | bytes 135200 | tf_op jit(solution)/shard_map/while/body/eval_jaxpr/ppermute | solution.py:12
  429.3 11.2 %conditional.13 = (bf16[1,33,2048]{2,1,0:T(8,128)(2,1)S(1)}, bf16[1,33,2048]{2,1,0:T(8,128)(2,1)S(1)}) conditional(s32[]{:T(128)} %convert_element_type.140, bf16[1,33,2048]{2,1,0:T(8,128)(2,1)S(1)} %get-tuple-element.965, (bf16[1,33,2048]{2,1,0:T(8,128)(2,1)S(1)}, s32[]{:T(128)}, bf16[6,1,33,2048]{3,2,1,0:T(8,128)(2,1)S(1)}, ...), branch_computations={%region_12.12_spmd, %region_13.14_spmd} | conditional | flops 554866688 | bytes 19681334 | solution.py:163
  442.8 15.0 %collective-permute-done.1 = bf16[1,33,2048]{2,1,0:T(8,128)(2,1)S(1)} collective-permute-done((bf16[1,33,2048]{2,1,0:T(8,128)(2,1)S(1)}, bf16[1,33,2048]{2,1,0:T(8,128)(2,1)S(1)}, u32[]{:S(2)}, u32[]{:S(2)}) %collective-permute-start.1) | collective-permute-done | bytes 135200 | tf_op jit(solution)/shard_map/while/body/eval_jaxpr/ppermute | solution.py:12
  458.4 11.2 %conditional.13 = (bf16[1,33,2048]{2,1,0:T(8,128)(2,1)S(1)}, bf16[1,33,2048]{2,1,0:T(8,128)(2,1)S(1)}) conditional(s32[]{:T(128)} %convert_element_type.140, bf16[1,33,2048]{2,1,0:T(8,128)(2,1)S(1)} %get-tuple-element.965, (bf16[1,33,2048]{2,1,0:T(8,128)(2,1)S(1)}, s32[]{:T(128)}, bf16[6,1,33,2048]{3,2,1,0:T(8,128)(2,1)S(1)}, ...), branch_computations={%region_12.12_spmd, %region_13.14_spmd} | conditional | flops 554866688 | bytes 19681334 | solution.py:163
  479.4 48.6 %reduce-scatter.7.cloned.1.call-done = bf16[256,1024]{1,0:T(8,128)(2,1)} async-done(((bf16[2048,1024]{1,0:T(8,128)(2,1)}), bf16[256,1024]{1,0:T(8,128)(2,1)}) %reduce-scatter.7.cloned.1.call-update) | async-done | bytes 524304 | tf_op jit(solution)/shard_map/reduce_scatter | solution.py:197
  535.2 15.4 %psum.15 = bf16[]{:T(256)} all-reduce(f32[]{:T(128)} %get-tuple-element.664), channel_id=1, replica_groups=mesh['dp'=2,'section'=4,'mp'=4] {'dp','mp'}, use_global_device_ids=true, to_apply=%region_21.22 | all-reduce | flops 1 | bytes 6 | tf_op jit(solution)/shard_map/psum | solution.py:203
  551.2 12.1 %all-reduce.1 = bf16[1,4]{1,0:T(2,128)(2,1)S(1)} all-reduce(bf16[1,4]{1,0:T(2,128)(2,1)S(1)} %broadcast_in_dim.72), channel_id=5, replica_groups=mesh['dp'=2,'section'=4,'mp'=4] {'section'}, use_global_device_ids=true, to_apply=%region_22.23.clone | all-reduce | flops 4 | bytes 16
  566.2 59.3 %reduce-scatter.5.cloned.1.call-done = bf16[256,2048]{1,0:T(8,128)(2,1)} async-done(((bf16[2048,2048]{1,0:T(8,128)(2,1)}), bf16[256,2048]{1,0:T(8,128)(2,1)}) %reduce-scatter.5.cloned.1.call-update) | async-done | bytes 1048592 | tf_op jit(solution)/shard_map/reduce_scatter | solution.py:182
  (296 shorter events, 291.1 us)
Async XLA Ops:
  13.1 6.0 copy-start.3
  13.1 104.6 %copy-start.1 = (bf16[512,2048]{1,0:T(8,128)(2,1)S(1)}, bf16[512,2048]{1,0:T(8,128)(2,1)}, u32[]{:S(2)}) copy-start(bf16[512,2048]{1,0:T(8,128)(2,1)} %param.29) | copy-start | bytes 6291460
  13.1 102.7 %all-to-all-start = ((bf16[4,512,2048]{2,1,0:T(8,128)(2,1)}), bf16[4,512,2048]{2,1,0:T(8,128)(2,1)}, u32[]{:S(2)}, u32[]{:S(2)}) async-start(bf16[4,512,2048]{2,1,0:T(8,128)(2,1)} %stack.3), calls=%async_computation | async-start | bytes 16777216 | tf_op jit(solution)/shard_map/all_to_all | solution.py:63
  18.9 509.2 %reduce-scatter.7.cloned.1.call-start = ((), (), s32[]{:S(2)}) async-start(), calls=%async_computation.5 | async-start | bytes 4718592 | tf_op jit(solution)/shard_map/reduce_scatter | solution.py:197
  128.1 4.1 collective-permute-start
  142.7 4.1 collective-permute-start
  157.3 4.1 collective-permute-start
  171.9 4.1 collective-permute-start
  186.5 4.1 collective-permute-start
  201.1 4.1 collective-permute-start
  210.7 7.9 %collective-permute-start = (bf16[1,33,2048]{2,1,0:T(8,128)(2,1)S(1)}, bf16[1,33,2048]{2,1,0:T(8,128)(2,1)}, u32[]{:S(2)}, u32[]{:S(2)}) collective-permute-start(bf16[1,33,2048]{2,1,0:T(8,128)(2,1)S(1)} %get-tuple-element.1090), channel_id=1, source_target_pairs={{0,4},{4,8},{8,12},{1,5},{5,9},{9,13},{2,6},{6,10},{10,14},{3,7},{... | collective-permute-start | bytes 405512 | tf_op jit(solution)/shard_map/while/body/eval_jaxpr/ppermute | solution.py:12
  224.0 4.1 collective-permute-start
  233.5 5.1 collective-permute-start
  239.6 8.3 %collective-permute-start.1 = (bf16[1,33,2048]{2,1,0:T(8,128)(2,1)S(1)}, bf16[1,33,2048]{2,1,0:T(8,128)(2,1)S(1)}, u32[]{:S(2)}, u32[]{:S(2)}) collective-permute-start(bf16[1,33,2048]{2,1,0:T(8,128)(2,1)S(1)} %get-tuple-element.966), channel_id=1, source_target_pairs={{4,0},{8,4},{12,8},{5,1},{9,5},{13,9},{6,2},{10,6},{14,10},{7,3},{... | collective-permute-start | bytes 405512 | tf_op jit(solution)/shard_map/while/body/eval_jaxpr/ppermute | solution.py:12
  248.5 8.8 %collective-permute-start.1 = (bf16[1,33,2048]{2,1,0:T(8,128)(2,1)S(1)}, bf16[1,33,2048]{2,1,0:T(8,128)(2,1)S(1)}, u32[]{:S(2)}, u32[]{:S(2)}) collective-permute-start(bf16[1,33,2048]{2,1,0:T(8,128)(2,1)S(1)} %get-tuple-element.966), channel_id=1, source_target_pairs={{4,0},{8,4},{12,8},{5,1},{9,5},{13,9},{6,2},{10,6},{14,10},{7,3},{... | collective-permute-start | bytes 405512 | tf_op jit(solution)/shard_map/while/body/eval_jaxpr/ppermute | solution.py:12
  258.0 53.9 %collective-permute-start.1 = (bf16[1,33,2048]{2,1,0:T(8,128)(2,1)S(1)}, bf16[1,33,2048]{2,1,0:T(8,128)(2,1)S(1)}, u32[]{:S(2)}, u32[]{:S(2)}) collective-permute-start(bf16[1,33,2048]{2,1,0:T(8,128)(2,1)S(1)} %get-tuple-element.966), channel_id=1, source_target_pairs={{4,0},{8,4},{12,8},{5,1},{9,5},{13,9},{6,2},{10,6},{14,10},{7,3},{... | collective-permute-start | bytes 405512 | tf_op jit(solution)/shard_map/while/body/eval_jaxpr/ppermute | solution.py:12
  323.8 17.3 %collective-permute-start.1 = (bf16[1,33,2048]{2,1,0:T(8,128)(2,1)S(1)}, bf16[1,33,2048]{2,1,0:T(8,128)(2,1)S(1)}, u32[]{:S(2)}, u32[]{:S(2)}) collective-permute-start(bf16[1,33,2048]{2,1,0:T(8,128)(2,1)S(1)} %get-tuple-element.966), channel_id=1, source_target_pairs={{4,0},{8,4},{12,8},{5,1},{9,5},{13,9},{6,2},{10,6},{14,10},{7,3},{... | collective-permute-start | bytes 405512 | tf_op jit(solution)/shard_map/while/body/eval_jaxpr/ppermute | solution.py:12
  353.0 17.3 %collective-permute-start.1 = (bf16[1,33,2048]{2,1,0:T(8,128)(2,1)S(1)}, bf16[1,33,2048]{2,1,0:T(8,128)(2,1)S(1)}, u32[]{:S(2)}, u32[]{:S(2)}) collective-permute-start(bf16[1,33,2048]{2,1,0:T(8,128)(2,1)S(1)} %get-tuple-element.966), channel_id=1, source_target_pairs={{4,0},{8,4},{12,8},{5,1},{9,5},{13,9},{6,2},{10,6},{14,10},{7,3},{... | collective-permute-start | bytes 405512 | tf_op jit(solution)/shard_map/while/body/eval_jaxpr/ppermute | solution.py:12
  382.1 17.3 %collective-permute-start.1 = (bf16[1,33,2048]{2,1,0:T(8,128)(2,1)S(1)}, bf16[1,33,2048]{2,1,0:T(8,128)(2,1)S(1)}, u32[]{:S(2)}, u32[]{:S(2)}) collective-permute-start(bf16[1,33,2048]{2,1,0:T(8,128)(2,1)S(1)} %get-tuple-element.966), channel_id=1, source_target_pairs={{4,0},{8,4},{12,8},{5,1},{9,5},{13,9},{6,2},{10,6},{14,10},{7,3},{... | collective-permute-start | bytes 405512 | tf_op jit(solution)/shard_map/while/body/eval_jaxpr/ppermute | solution.py:12
  411.3 17.3 %collective-permute-start.1 = (bf16[1,33,2048]{2,1,0:T(8,128)(2,1)S(1)}, bf16[1,33,2048]{2,1,0:T(8,128)(2,1)S(1)}, u32[]{:S(2)}, u32[]{:S(2)}) collective-permute-start(bf16[1,33,2048]{2,1,0:T(8,128)(2,1)S(1)} %get-tuple-element.966), channel_id=1, source_target_pairs={{4,0},{8,4},{12,8},{5,1},{9,5},{13,9},{6,2},{10,6},{14,10},{7,3},{... | collective-permute-start | bytes 405512 | tf_op jit(solution)/shard_map/while/body/eval_jaxpr/ppermute | solution.py:12
  440.5 17.3 %collective-permute-start.1 = (bf16[1,33,2048]{2,1,0:T(8,128)(2,1)S(1)}, bf16[1,33,2048]{2,1,0:T(8,128)(2,1)S(1)}, u32[]{:S(2)}, u32[]{:S(2)}) collective-permute-start(bf16[1,33,2048]{2,1,0:T(8,128)(2,1)S(1)} %get-tuple-element.966), channel_id=1, source_target_pairs={{4,0},{8,4},{12,8},{5,1},{9,5},{13,9},{6,2},{10,6},{14,10},{7,3},{... | collective-permute-start | bytes 405512 | tf_op jit(solution)/shard_map/while/body/eval_jaxpr/ppermute | solution.py:12
  469.7 7.2 %collective-permute-start.1 = (bf16[1,33,2048]{2,1,0:T(8,128)(2,1)S(1)}, bf16[1,33,2048]{2,1,0:T(8,128)(2,1)S(1)}, u32[]{:S(2)}, u32[]{:S(2)}) collective-permute-start(bf16[1,33,2048]{2,1,0:T(8,128)(2,1)S(1)} %get-tuple-element.966), channel_id=1, source_target_pairs={{4,0},{8,4},{12,8},{5,1},{9,5},{13,9},{6,2},{10,6},{14,10},{7,3},{... | collective-permute-start | bytes 405512 | tf_op jit(solution)/shard_map/while/body/eval_jaxpr/ppermute | solution.py:12
  479.4 85.2 %reduce-scatter.9.cloned.1.call-start = ((), (), s32[]{:S(2)}) async-start(), calls=%async_computation.6 | async-start | bytes 655360 | tf_op jit(solution)/shard_map/reduce_scatter | solution.py:206
  528.1 97.4 %reduce-scatter.5.cloned.1.call-start = ((), (), s32[]{:S(2)}) async-start(), calls=%async_computation.4 | async-start | bytes 9437184 | tf_op jit(solution)/shard_map/reduce_scatter | solution.py:182
  (2 other events, 6.5 us)
Sparse Core Ops, SparseCore 0:
  479.5 48.5 reduce-scatter.6
  530.3 21.8 reduce-scatter.8
  555.7 69.7 reduce-scatter.4
